TPU v7x, 32 devices: a whole 2x2x4 slice. The times are simulated.
32 devices in a mesh: rep: 4 (over y, x), shard: 8 (over z, core).
Axes of the slice: x: 2, y: 2, z: 4, core: 2. Of those that a mesh axis runs over, the one named last changes fastest.
Arguments:
- hot_ids: int32 [65536], P(('rep', 'shard')), may hold values from 0 to 8191
- hot_grads: bfloat16 [65536, 128], P(('rep', 'shard')), may hold values from -6 to 6
- hot_rows: float32 [8192, 128], replicated, may hold values from -6 to 6
- hot_accum: float32 [8192], replicated, may hold values from 0.5 to 4
- cold_counts: int32 [32, 32], P(('rep', 'shard')), may hold values from 1 to 16, as said below
- cold_slots: int32 [32, 32, 16], P(('rep', 'shard')), may hold values from 0 to 8191
- cold_grads: bfloat16 [32, 32, 16, 128], P(('rep', 'shard')), may hold values from -6 to 6
- cold_rows: float32 [262144, 128], P(('rep', 'shard')), may hold values from -6 to 6
- cold_accum: float32 [262144], P(('rep', 'shard')), may hold values from 0.5 to 4
Outputs:
- new_hot_rows: float32 [8192, 128], replicated
- new_hot_accum: float32 [8192], replicated
- new_cold_rows: float32 [262144, 128], P(('rep', 'shard'))
- new_cold_accum: float32 [262144], P(('rep', 'shard'))
Inputs may be any that keep to these rules, and one draw needn't show every extreme that they name: `cold_counts`: every entry is at least 1 and at most 16; in every draw some owner receives 16 live slots from every sender.
All inputs are finite; a program needn't handle non-finite values.
Results may differ from a plain program's by a relative error of at most 0.0003.
Values may be sent and summed in bfloat16 or wider, within the bound.
A program may use at most 128 MiB of HBM per device.

v0:
```python
import functools

import jax
import jax.numpy as jnp
from jax import lax
from jax.experimental import pallas as pl
from jax.experimental.pallas import tpu as pltpu
from jax.sharding import PartitionSpec as P

learn_rate = 0.5
LANES = 128
PAD = 8
BOTH = ("rep", "shard")


def adagrad(rows, accum_row, grad):
    m = rows.shape[0]
    diag = lax.broadcasted_iota(jnp.int32, (m, LANES), 0) == lax.broadcasted_iota(
        jnp.int32, (m, LANES), 1
    )
    square = jnp.sum(grad * grad, axis=1, keepdims=True) * (1.0 / grad.shape[1])
    accum = jnp.sum(jnp.where(diag, accum_row, 0.0), axis=1, keepdims=True)
    accum_new = accum + square
    rows_new = rows - grad * (learn_rate / jnp.sqrt(accum_new))
    accum_new_row = jnp.sum(jnp.where(diag, accum_new, 0.0), axis=0, keepdims=True)
    return rows_new, accum_new_row


def onehot_dot(ids, base, rows, grads):
    lookups = ids.shape[1]
    row = lax.broadcasted_iota(jnp.int32, (rows, lookups), 0)
    hit = jnp.where(row == ids - base, 1.0, 0.0).astype(jnp.bfloat16)
    return jnp.dot(hit, grads, preferred_element_type=jnp.float32)


def kernel(
    reps, shards,
    ids, grads, hot_rows, hot_accum, cold_ids, cold_grads, cold_rows, cold_accum,
    hot_out, hot_accum_out, cold_out, cold_accum_out,
    hot_buf, ids_buf, grads_buf, acc, z_buf, rows_buf, cold_buf, cids_buf, cgrads_buf,
    raw_send, raw_recv, raw_core_send, raw_core_recv, z_send, z_recv,
    zg_send, zg_recv, rg_send, rg_recv, core_send, core_recv,
    cold_send, cold_recv, local_sem, out_sem,
):
    total = reps * shards
    depth = shards // 2
    bits = reps.bit_length() - 1
    own_rows = acc.shape[1]
    half_rows = own_rows // 2
    rep, shard = lax.axis_index("rep"), lax.axis_index("shard")
    z, core = shard // 2, shard % 2
    me = rep * shards + shard
    partner = {"rep": rep, "shard": z * 2 + 1 - core}

    def flip(r, bit):
        m = 1 << bit
        return r + m * (1 - 2 * ((r // m) % 2))

    def across(d):
        r = 0
        for k in range(depth.bit_length() - 1):
            r += (1 << k) * ((z // (1 << k) + d // (1 << k)) % 2)
        return r

    orders = (tuple(range(bits)), tuple(reversed(range(bits))))

    def origin(h, i):
        r = rep
        for k in range(bits):
            if (i >> k) & 1:
                r = flip(r, orders[h][k])
        return r

    def remote(src, dst, s_sem, r_sem, device):
        return pltpu.make_async_remote_copy(
            src_ref=src, dst_ref=dst, send_sem=s_sem, recv_sem=r_sem,
            device_id=device, device_id_type=pl.DeviceIdType.MESH,
        )

    chunk = (core * reps + rep) * depth + z
    loads = [
        pltpu.make_async_copy(cold_rows, cold_buf, local_sem.at[0]),
        pltpu.make_async_copy(hot_rows.at[pl.ds(2 * chunk, 2)], rows_buf, local_sem.at[1]),
        pltpu.make_async_copy(cold_ids.at[me], cids_buf.at[me], local_sem.at[2]),
        pltpu.make_async_copy(cold_grads.at[me], cgrads_buf.at[me], local_sem.at[3]),
    ]
    for copy in loads:
        copy.start()

    barrier = pltpu.get_barrier_semaphore()

    @pl.loop(1, total)
    def _(d):
        p = (me + d) % total
        pl.semaphore_signal(
            barrier, inc=1, device_id={"rep": p // shards, "shard": p % shards},
            device_id_type=pl.DeviceIdType.MESH,
        )

    pl.semaphore_wait(barrier, total - 1)

    sends = []
    arrivals = {}

    def raw_ref(h, i):
        if i == 0:
            return ids.at[h], grads.at[h]
        return ids_buf.at[0, h, i], grads_buf.at[0, h, i]

    def top(i):
        return i.bit_length() - 1

    def relay(h, i, q):
        j = i | (1 << q)
        device = {"rep": flip(rep, orders[h][q]), "shard": shard}
        pair = []
        for k, (src, buf) in enumerate(zip(raw_ref(h, i), (ids_buf, grads_buf))):
            slot = (h * reps + j) * 2 + k
            pair.append(remote(src, buf.at[0, h, j], raw_send.at[slot], raw_recv.at[slot], device))
        for copy in pair:
            copy.start()
            sends.append(copy)
        arrivals[h, j] = pair

    core_pairs = {}

    def cross(h, i):
        pair = []
        for k, (src, buf) in enumerate(zip(raw_ref(h, i), (ids_buf, grads_buf))):
            slot = (h * reps + i) * 2 + k
            pair.append(
                remote(src, buf.at[1, h, i], raw_core_send.at[slot], raw_core_recv.at[slot], partner)
            )
        for copy in pair:
            copy.start()
            sends.append(copy)
        core_pairs[h, i] = pair

    for q in range(bits):
        for h in range(2):
            relay(h, 0, q)
    for h in range(2):
        cross(h, 0)

    @pl.loop(1, total)
    def _(d):
        p = (me + d) % total
        device = {"rep": p // shards, "shard": p % shards}
        remote(cold_ids.at[p], cids_buf.at[me], cold_send.at[0], cold_recv.at[0], device).start()
        remote(cold_grads.at[p], cgrads_buf.at[me], cold_send.at[1], cold_recv.at[1], device).start()

    share = (core * reps + rep) * depth

    def block_sum(c, i, base):
        value = None
        for h in range(2):
            ids_ref, grads_ref = raw_ref(h, i) if c == 0 else (ids_buf.at[1, h, i], grads_buf.at[1, h, i])
            part = onehot_dot(ids_ref[...], base, own_rows, grads_ref[...])
            value = part if value is None else value + part
        return value

    def z_copy(d, zc):
        target = {"rep": rep, "shard": zc * 2 + core}
        return remote(acc.at[zc], z_buf.at[d - 1], z_send.at[d - 1], z_recv.at[d - 1], target)

    for i in range(reps):
        if i > 0:
            for h in range(2):
                for copy in arrivals[h, i]:
                    copy.wait_recv()
                for q in range(top(i) + 1, bits):
                    relay(h, i, q)
                cross(h, i)
        for c in range(2):
            if c == 1:
                for h in range(2):
                    for copy in core_pairs[h, i]:
                        copy.wait_recv()
            last = i == reps - 1 and c == 1

            @pl.loop(1, depth + 1)
            def _(d):
                zc = across(d % depth)
                value = block_sum(c, i, (share + zc) * own_rows)
                if i == 0 and c == 0:
                    acc[zc] = value
                else:
                    acc[zc] += value
                if last:
                    @pl.when(d >= 2)
                    def _():
                        z_copy(d - 1, across(d - 1)).start()

    for copy in loads:
        copy.wait()
    for k, buf in enumerate((cids_buf, cgrads_buf)):
        part = buf.at[pl.ds(0, total - 1)]
        pltpu.make_async_copy(part, part, cold_recv.at[k]).wait()
    capacity = cgrads_buf.shape[1]
    group = LANES // capacity
    cold_id_row = jnp.concatenate(
        [jnp.sum(cids_buf[g * group:(g + 1) * group], axis=0) for g in range(total // group)], axis=1
    ) - 1

    step_rows = 2 * LANES

    @pl.loop(0, cold_buf.shape[0] // step_rows)
    def _(b):
        terms = cgrads_buf[...].reshape(total * capacity, LANES)
        grad = onehot_dot(cold_id_row, b * step_rows, step_rows, terms)
        for s in range(2):
            at = pl.ds(pl.multiple_of(b * step_rows + s * LANES, LANES), LANES)
            new_rows, new_accum = adagrad(
                cold_buf[at], cold_accum[2 * b + s], grad[s * LANES:(s + 1) * LANES]
            )
            cold_buf[at] = new_rows
            cold_accum_out[2 * b + s] = new_accum

    cold_copy = pltpu.make_async_copy(cold_buf, cold_out, out_sem.at[0])
    cold_copy.start()

    @pl.loop(1, depth)
    def _(d):
        z_copy(d, across(d)).wait_recv()

    for h in range(2):
        at = pl.ds(h * half_rows, half_rows)
        grad = acc[z, at]
        for d in range(1, depth):
            grad += z_buf[d - 1, at]
        new_rows, new_accum = adagrad(rows_buf[h], hot_accum[2 * chunk + h], grad)
        hot_buf[2 * chunk + h, pl.ds(0, half_rows)] = new_rows
        hot_buf[2 * chunk + h, pl.ds(half_rows, PAD)] = jnp.broadcast_to(new_accum, (PAD, LANES))

    def zg_copy(d):
        target = {"rep": rep, "shard": across(d) * 2 + core}
        part = hot_buf.at[pl.ds(2 * chunk, 2)]
        return remote(part, part, zg_send.at[d - 1], zg_recv.at[d - 1], target)

    for d in range(1, depth):
        zg_copy(d).start()

    gathered = {}

    def out_block(d, h, i, side_of=core):
        zc = across(d)
        return 2 * ((side_of * reps + origin(h, i)) * depth + zc) + h

    def publish(block):
        pltpu.make_async_copy(
            hot_buf.at[block, pl.ds(0, half_rows)], hot_out.at[block], out_sem.at[1]
        ).start()

    def spread(d, h, i):
        part = hot_buf.at[out_block(d, h, i)]
        for q in range(top(i) + 1, bits):
            j = i | (1 << q)
            slot = (d * 2 + h) * reps + j
            device = {"rep": flip(rep, orders[h][q]), "shard": shard}
            copy = remote(part, part, rg_send.at[slot], rg_recv.at[slot], device)
            copy.start()
            sends.append(copy)
            gathered[d, h, j] = copy
        slot = (d * 2 + h) * reps + i
        copy = remote(part, part, core_send.at[slot], core_recv.at[slot], partner)
        copy.start()
        sends.append(copy)
        publish(out_block(d, h, i))

    def finish(d):
        for i in range(1, reps):
            for h in range(2):
                part = hot_buf.at[out_block(d, h, i)]
                slot = (d * 2 + h) * reps + i
                remote(part, part, rg_send.at[slot], rg_recv.at[slot], partner).wait_recv()
                spread(d, h, i)

    def crossed(d):
        for i in range(reps):
            for h in range(2):
                block = out_block(d, h, i, 1 - core)
                part = hot_buf.at[block]
                slot = (d * 2 + h) * reps + i
                remote(part, part, core_send.at[slot], core_recv.at[slot], partner).wait_recv()
                publish(block)

    for d in range(depth):
        if d > 0:
            zg_copy(d).wait_recv()
        for h in range(2):
            spread(d, h, 0)
        if d > 0:
            finish(d - 1)
        if d > 1:
            crossed(d - 2)
    finish(depth - 1)
    for d in range(max(depth - 2, 0), depth):
        crossed(d)

    @pl.loop(0, 2 * total)
    def _(b):
        hot_accum_out[b] = hot_buf[b, pl.ds(half_rows, 1)]

    for copy in sends:
        copy.wait_send()
    for d in range(1, depth):
        z_copy(d, across(d)).wait_send()
        zg_copy(d).wait_send()
    for k, buf in enumerate((cold_ids, cold_grads)):
        part = buf.at[pl.ds(0, total - 1)]
        pltpu.make_async_copy(part, part, cold_send.at[k]).wait()
    cold_copy.wait()
    pltpu.make_async_copy(hot_out, hot_out, out_sem.at[1]).wait()


def local(
    hot_ids, hot_grads, hot_rows, hot_accum, cold_counts, cold_slots, cold_grads, cold_rows, cold_accum
):
    reps, shards = lax.axis_size("rep"), lax.axis_size("shard")
    total, depth = reps * shards, shards // 2
    assert reps & (reps - 1) == 0 and shards & (shards - 1) == 0
    hot_count, width = hot_rows.shape
    lookups = hot_ids.shape[0]
    own_rows = hot_count // total
    half_rows = own_rows // 2
    cold_count = cold_rows.shape[0]
    capacity = cold_slots.shape[2]
    assert width == LANES and half_rows <= LANES and LANES % capacity == 0

    half = lookups // 2
    accum_blocks = hot_accum.reshape(2 * total, 1, half_rows)
    if half_rows < LANES:
        accum_blocks = jnp.pad(accum_blocks, ((0, 0), (0, 0), (0, LANES - half_rows)))
    group = LANES // capacity
    me = lax.axis_index("rep") * shards + lax.axis_index("shard")
    lane = lax.broadcasted_iota(jnp.int32, (total, 1, LANES), 2)
    live = (lane // capacity == me % group) & (lane % capacity < cold_counts.reshape(total, 1, 1))
    slot_lanes = jnp.tile(cold_slots.reshape(total, 1, capacity), (1, 1, group))
    cold_ids = jnp.where(live, slot_lanes + 1, 0)

    f32, i32, bf16 = jnp.float32, jnp.int32, jnp.bfloat16
    vmem, anywhere = pl.BlockSpec(memory_space=pltpu.VMEM), pl.BlockSpec(memory_space=pl.ANY)
    dma = pltpu.SemaphoreType.DMA
    hot_out, hot_accum_out, cold_out, cold_accum_out = pl.pallas_call(
        functools.partial(kernel, reps, shards),
        out_shape=(
            jax.ShapeDtypeStruct((2 * total, half_rows, LANES), f32),
            jax.ShapeDtypeStruct((2 * total, 1, LANES), f32),
            jax.ShapeDtypeStruct((cold_count, LANES), f32),
            jax.ShapeDtypeStruct((cold_count // LANES, 1, LANES), f32),
        ),
        in_specs=[vmem, vmem, anywhere, vmem, vmem, vmem, anywhere, vmem],
        out_specs=(anywhere, vmem, anywhere, vmem),
        scratch_shapes=[
            pltpu.VMEM((2 * total, half_rows + PAD, LANES), f32),
            pltpu.VMEM((2, 2, reps, 1, half), i32),
            pltpu.VMEM((2, 2, reps, half, LANES), bf16),
            pltpu.VMEM((depth, own_rows, LANES), f32),
            pltpu.VMEM((max(depth - 1, 1), own_rows, LANES), f32),
            pltpu.VMEM((2, half_rows, LANES), f32),
            pltpu.VMEM((cold_count, LANES), f32),
            pltpu.VMEM((total, 1, LANES), i32),
            pltpu.VMEM((total, capacity, LANES), bf16),
            dma((4 * reps,)), dma((4 * reps,)), dma((4 * reps,)), dma((4 * reps,)),
            dma((depth,)), dma((depth,)), dma((depth,)), dma((depth,)),
            dma((2 * depth * reps,)), dma((2 * depth * reps,)),
            dma((2 * depth * reps,)), dma((2 * depth * reps,)),
            dma((2,)), dma((2,)), dma((4,)), dma((2,)),
        ],
        compiler_params=pltpu.CompilerParams(collective_id=0, has_side_effects=True),
    )(
        hot_ids.reshape(2, 1, half),
        hot_grads.reshape(2, half, LANES),
        hot_rows.reshape(2 * total, half_rows, LANES),
        accum_blocks,
        cold_ids,
        cold_grads.reshape(total, capacity, LANES),
        cold_rows,
        cold_accum.reshape(cold_count // LANES, 1, LANES),
    )
    return (
        hot_out.reshape(hot_count, LANES),
        hot_accum_out[:, 0, :half_rows].reshape(hot_count),
        cold_out,
        cold_accum_out.reshape(cold_count),
    )


def solution(mesh):
    placed = (
        P(BOTH), P(BOTH, None), P(), P(), P(BOTH, None), P(BOTH, None, None),
        P(BOTH, None, None, None), P(BOTH, None), P(BOTH),
    )
    return jax.shard_map(
        local,
        mesh=mesh,
        in_specs=placed,
        out_specs=(P(), P(), P(BOTH, None), P(BOTH)),
        check_vma=False,
    )
```

profile of v0, /device:TPU:0, one launch (start us, length us, event | category | flops | bytes accessed | tf_op | source)
XLA Modules:
  0.0 84.7 jit_solution(3037954233985548075)
XLA Ops:
  0.7 0.7 add_bitcast_fusion
  1.4 0.1 copy.14
  1.4 1.4 %and_select_fusion.cold_ids = s32[32,1,128]{2,1,0:T(1,128)} fusion(s32[32,1,128]{2,1,0:T(1,128)S(1)} %copy.14, pred[128]{0:T(512)(128)(4,1)S(1)} %get-tuple-element.13, pred[128]{0:T(512)(128)(4,1)S(1)} %get-tuple-element.12, s32[32]{0:T(128)} %bitcast.23, s32[128]{0:T(128)S(1)} %get-tuple-element.15, s32[128]{0:T(128)S(1)} %get-tuple-element.16, ...), kind=kLoop, calls=%fused_computation | loop fusion | flops 24576 | bytes 35204 | tf_op jit(solution)/shard_map/jit(_where)/select_n | solution.py:339
  2.8 74.0 %shard_map.120 = (f32[64,128,128]{2,1,0:T(8,128)}, f32[64,1,128]{2,1,0:T(1,128)}, f32[8192,128]{1,0:T(8,128)}, f32[64,1,128]{2,1,0:T(1,128)}) custom-call(s32[2,1,1024]{2,1,0:T(1,128)} %bitcast.22, bf16[2,1024,128]{2,1,0:T(8,128)(2,1)} %bitcast.15, f32[64,128,128]{2,1,0:T(8,128)} %bitcast.14, f32[64,1,128]{2,1,0:T(1,128)} %bitcast.18, ...), custom_call_target="tpu_custom_call" | custom-call | tf_op jit(solution)/shard_map/pallas_call | solution.py:344
  76.8 0.0 copy-start.2
  76.8 0.0 copy-start
  76.9 4.6 %copy.19 = f32[8192,128]{1,0:T(8,128)} copy(f32[8192,128]{1,0:T(8,128)} %bitcast.13) | data formatting | bytes 8388608
  81.5 0.0 copy-done.2
  81.5 0.6 copy.20
  82.1 0.0 copy-done
  82.1 0.0 copy-start.1
  82.1 2.0 %copy.21 = f32[8192,128]{1,0:T(8,128)} copy(f32[8192,128]{1,0:T(8,128)S(1)} %copy-done) | data formatting | bytes 8388608
  84.1 0.0 copy-done.1
  84.1 0.6 copy.22
  (4 shorter events, 0.0 us)
Async XLA Ops:
  76.8 4.6 %copy-start.2 = (f32[64,1,128]{2,1,0:T(1,128)S(1)}, f32[64,1,128]{2,1,0:T(1,128)}, u32[]{:S(2)}) copy-start(f32[64,1,128]{2,1,0:T(1,128)} %get-tuple-element.9) | copy-start | bytes 98308
  76.8 5.3 %copy-start = (f32[8192,128]{1,0:T(8,128)S(1)}, f32[8192,128]{1,0:T(8,128)}, u32[]{:S(2)}) copy-start(f32[8192,128]{1,0:T(8,128)} %get-tuple-element.24) | copy-start | bytes 12582916
  82.1 2.0 %copy-start.1 = (f32[64,1,128]{2,1,0:T(1,128)S(1)}, f32[64,1,128]{2,1,0:T(1,128)}, u32[]{:S(2)}) copy-start(f32[64,1,128]{2,1,0:T(1,128)} %get-tuple-element.11) | copy-start | bytes 98308
where the time goes:
time: 85.4 us; the launch traced here: 84.7 us
  Pallas kernels  74 us (87%)
  local copies, waits for them, and re-layouts  7.94 us (9%)
  other arithmetic  2.1 us (2%)
    pallas_call x1, Pallas kernels, local(): pl.pallas_call(functools.partial(kernel, reps, shards), out_shape=(jax.Sh...  74 us
    unnamed x10, local copies, waits for them, and re-layouts  7.88 us

commit v1 on v0

v1 whole, which is shorter than its diff:
```python
import functools

import jax
import jax.numpy as jnp
from jax import lax
from jax.experimental import pallas as pl
from jax.experimental.pallas import tpu as pltpu
from jax.sharding import PartitionSpec as P

learn_rate = 0.5
LANES = 128
UNITS = 8
TILE = 256
BOTH = ("rep", "shard")


def adagrad(rows, accum_row, grad):
    m = rows.shape[0]
    diag = lax.broadcasted_iota(jnp.int32, (m, LANES), 0) == lax.broadcasted_iota(
        jnp.int32, (m, LANES), 1
    )
    square = jnp.sum(grad * grad, axis=1, keepdims=True) * (1.0 / grad.shape[1])
    accum = jnp.sum(jnp.where(diag, accum_row, 0.0), axis=1, keepdims=True)
    accum_new = accum + square
    rows_new = rows - grad * (learn_rate / jnp.sqrt(accum_new))
    accum_new_row = jnp.sum(jnp.where(diag, accum_new, 0.0), axis=0, keepdims=True)
    return rows_new, accum_new_row


def onehot_dot(ids, base, rows, grads):
    lookups = ids.shape[1]
    row = lax.broadcasted_iota(jnp.int32, (rows, lookups), 0)
    hit = jnp.where(row == ids - base, 1.0, 0.0).astype(jnp.bfloat16)
    return jnp.dot(hit, grads, preferred_element_type=jnp.float32)


def log2(n):
    return n.bit_length() - 1


def unit_orders(rep_bits, depth_bits):
    across = [("rep", b) for b in range(rep_bits)]
    along = [("depth", b) for b in range(depth_bits)]
    back = across[::-1]
    first = [across + along, back + along]
    third = [along[:1] + across + along[1:], along[:1] + back + along[1:]]
    kinds = [first[0], first[1], third[0], first[0], first[1], third[1], first[0], first[1]]
    return [kinds[u % len(kinds)] for u in range(UNITS)]


def plan(steps):
    stages = 2 * steps + 3
    events = []
    for u in range(UNITS):
        for s in range(stages):
            events.append((2.0 * u + 3.0 * s, s, u))
    for c in range(UNITS):
        events.append((14.0 + 2.0 * c, -1, c))
    return [(s, u) for _, s, u in sorted(events)]


def kernel(
    reps, shards,
    ids, grads, hot_rows, hot_accum, slots, counts, cold_grads, cold_rows, cold_accum,
    hot_out, hot_accum_out, cold_out, cold_accum_out,
    ids_buf, grads_buf, acc, rs_buf, sums, hot_acc_buf, cold_acc_buf, slots_buf, counts_buf,
    cold_own, cold_ids, cids_buf, cgrads_buf,
    load_sem, raw_send, raw_recv, rs_send, rs_recv, ag_send, ag_recv, cross_send, cross_recv,
    cold_send, cold_recv,
):
    total = reps * shards
    depth = shards // 2
    groups = reps * depth
    steps = log2(groups)
    unit_rows = acc.shape[1]
    own = unit_rows // groups
    blocks = unit_rows // LANES
    rep, shard = lax.axis_index("rep"), lax.axis_index("shard")
    z, core = shard // 2, shard % 2
    me = rep * shards + shard
    partner = {"rep": rep, "shard": z * 2 + 1 - core}
    orders = unit_orders(log2(reps), log2(depth))

    def bit_of(dim):
        kind, b = dim
        return ((rep if kind == "rep" else z) // (1 << b)) % 2

    def neighbour(dim):
        kind, b = dim
        move = (1 << b) * (1 - 2 * bit_of(dim))
        if kind == "rep":
            return {"rep": rep + move, "shard": shard}
        return {"rep": rep, "shard": (z + move) * 2 + core}

    def remote(src, dst, s_sem, r_sem, device):
        return pltpu.make_async_remote_copy(
            src_ref=src, dst_ref=dst, send_sem=s_sem, recv_sem=r_sem,
            device_id=device, device_id_type=pl.DeviceIdType.MESH,
        )

    loads = [
        pltpu.make_async_copy(src, dst, load_sem.at[k])
        for k, (src, dst) in enumerate((
            (ids, ids_buf.at[0]), (grads, grads_buf.at[0]), (slots, slots_buf), (counts, counts_buf),
            (cold_grads, cold_own), (cold_grads.at[me], cgrads_buf.at[me]), (cold_rows, cold_out),
            (hot_rows, hot_out), (hot_accum, hot_acc_buf), (cold_accum, cold_acc_buf),
        ))
    ]
    for copy in loads:
        copy.start()

    barrier = pltpu.get_barrier_semaphore()

    @pl.loop(1, total)
    def _(d):
        p = (me + d) % total
        pl.semaphore_signal(
            barrier, inc=1, device_id={"rep": p // shards, "shard": p % shards},
            device_id_type=pl.DeviceIdType.MESH,
        )

    tiles = unit_rows // TILE

    def partial_sum(src, tile):
        base = core * (UNITS * unit_rows) + tile * TILE
        return onehot_dot(ids_buf[src], base, TILE, grads_buf[src])

    def own_part(first, last):
        @pl.loop(first * tiles, last * tiles)
        def _(t):
            acc[t // tiles, pl.ds(pl.multiple_of((t % tiles) * TILE, TILE), TILE)] = partial_sum(0, t)

    def partner_part(u):
        @pl.loop(0, tiles)
        def _(t):
            acc[u, pl.ds(pl.multiple_of(t * TILE, TILE), TILE)] += partial_sum(1, u * tiles + t)

    for copy in loads[:2]:
        copy.wait()
    own_part(0, UNITS // 2)

    capacity = slots_buf.shape[0]
    group = LANES // capacity
    for copy in loads[2:6]:
        copy.wait()
    slot = lax.broadcasted_iota(jnp.int32, (capacity, total), 0)
    live = jnp.where(slot < counts_buf[...], slots_buf[...] + 1, 0)
    lane_group = lax.broadcasted_iota(jnp.int32, (LANES, total), 0) // capacity
    spread = jnp.where(lane_group == me % group, jnp.concatenate([live] * group, axis=0), 0)
    cold_ids[...] = jnp.transpose(spread).reshape(total, 1, LANES)
    cids_buf[me] = cold_ids[me]

    pl.semaphore_wait(barrier, total - 1)

    raw = [
        remote(buf.at[0], buf.at[1], raw_send.at[k], raw_recv.at[k], partner)
        for k, buf in enumerate((ids_buf, grads_buf))
    ]
    for copy in raw:
        copy.start()

    @pl.loop(1, total)
    def _(d):
        p = (me + d) % total
        device = {"rep": p // shards, "shard": p % shards}
        remote(cold_ids.at[p], cids_buf.at[me], cold_send.at[0], cold_recv.at[0], device).start()
        remote(cold_own.at[p], cgrads_buf.at[me], cold_send.at[1], cold_recv.at[1], device).start()

    own_part(UNITS // 2, UNITS)
    for copy in raw:
        copy.wait_recv()

    ranges = []
    for order in orders:
        low, size, found = 0, groups, []
        for dim in order:
            size //= 2
            bit = bit_of(dim)
            mine = low + size * bit
            found.append((mine, low + size * (1 - bit), size))
            low = mine
        ranges.append(found)

    def span(start, size):
        return pl.ds(pl.multiple_of(start * own, own), size * own)

    def rs_copy(u, s):
        _, other, size = ranges[u][s]
        k = u * steps + s
        return remote(
            acc.at[u, span(other, size)], rs_buf.at[u, pl.ds(unit_rows - 2 * size * own, size * own)],
            rs_send.at[k], rs_recv.at[k], neighbour(orders[u][s]),
        )

    def block_of(u):
        return core * UNITS + u

    def ag_copy(u, s, arriving=False):
        mine, other, size = ranges[u][s]
        k = u * steps + s
        part = sums.at[block_of(u), span(other if arriving else mine, size)]
        return remote(part, part, ag_send.at[k], ag_recv.at[k], neighbour(orders[u][s]))

    def cross_copy(u, half, arriving=False):
        mine, other, size = ranges[u][0]
        block = (1 - core) * UNITS + u if arriving else block_of(u)
        part = sums.at[block, span((mine, other)[half], size)]
        k = 2 * u + half
        return remote(part, part, cross_send.at[k], cross_recv.at[k], partner)

    def update(block):
        @pl.loop(0, blocks)
        def _(j):
            at = block * blocks + j
            grad = sums[block, pl.ds(pl.multiple_of(j * LANES, LANES), LANES)]
            new_rows, new_accum = adagrad(hot_out[at], hot_acc_buf[at], grad)
            hot_out[at] = new_rows
            hot_accum_out[at] = new_accum

    sends = []

    def send(copy):
        copy.start()
        sends.append(copy)

    cold_steps = cold_out.shape[0] // TILE
    per_tile = TILE // LANES

    def cold_part(c):
        if c == 0:
            for copy in loads[6:]:
                copy.wait()
            for k, buf in enumerate((cids_buf, cgrads_buf)):
                part = buf.at[pl.ds(0, total - 1)]
                pltpu.make_async_copy(part, part, cold_recv.at[k]).wait()
        row = jnp.concatenate(
            [jnp.sum(cids_buf[g * group:(g + 1) * group], axis=0) for g in range(total // group)],
            axis=1,
        ) - 1

        @pl.loop(c * cold_steps // UNITS, (c + 1) * cold_steps // UNITS)
        def _(b):
            terms = cgrads_buf[...].reshape(total * capacity, LANES)
            grad = onehot_dot(row, b * TILE, TILE, terms)
            for s in range(per_tile):
                at = pl.ds(pl.multiple_of(b * TILE + s * LANES, LANES), LANES)
                new_rows, new_accum = adagrad(
                    cold_out[at], cold_acc_buf[per_tile * b + s], grad[s * LANES:(s + 1) * LANES]
                )
                cold_out[at] = new_rows
                cold_accum_out[per_tile * b + s] = new_accum

    def stage(s, u):
        if s == 0:
            partner_part(u)
            send(rs_copy(u, 0))
        elif s <= steps:
            rs_copy(u, s - 1).wait_recv()
            mine, _, size = ranges[u][s - 1]
            at = span(mine, size)
            arrived = rs_buf[u, pl.ds(unit_rows - 2 * size * own, size * own)]
            if s < steps:
                acc[u, at] += arrived
                send(rs_copy(u, s))
            else:
                sums[block_of(u), at] = acc[u, at] + arrived
                send(ag_copy(u, steps - 1))
        elif s < 2 * steps:
            ag_copy(u, 2 * steps - s, True).wait_recv()
            send(ag_copy(u, 2 * steps - 1 - s))
            if s == 2 * steps - 1:
                send(cross_copy(u, 0))
        elif s == 2 * steps:
            ag_copy(u, 0, True).wait_recv()
            send(cross_copy(u, 1))
        elif s == 2 * steps + 1:
            update(block_of(u))
        else:
            for half in range(2):
                cross_copy(u, half, True).wait_recv()
            update((1 - core) * UNITS + u)

    for s, u in plan(steps):
        if s < 0:
            cold_part(u)
        else:
            stage(s, u)

    for copy in raw + sends:
        copy.wait_send()
    for k, buf in enumerate((cold_ids, cold_own)):
        part = buf.at[pl.ds(0, total - 1)]
        pltpu.make_async_copy(part, part, cold_send.at[k]).wait()


def flush(hot, hot_accum, cold, cold_accum, hot_out, hot_accum_out, cold_out, cold_accum_out, sem):
    copies = [
        pltpu.make_async_copy(src, dst, sem.at[k])
        for k, (src, dst) in enumerate((
            (hot, hot_out), (cold, cold_out), (hot_accum, hot_accum_out), (cold_accum, cold_accum_out),
        ))
    ]
    for copy in copies:
        copy.start()
    for copy in copies:
        copy.wait()


def local(
    hot_ids, hot_grads, hot_rows, hot_accum, cold_counts, cold_slots, cold_grads, cold_rows, cold_accum
):
    reps, shards = lax.axis_size("rep"), lax.axis_size("shard")
    total, groups = reps * shards, reps * shards // 2
    assert reps & (reps - 1) == 0 and shards & (shards - 1) == 0
    steps = log2(groups)
    hot_count, width = hot_rows.shape
    lookups = hot_ids.shape[0]
    unit_rows = hot_count // (2 * UNITS)
    cold_count = cold_rows.shape[0]
    capacity = cold_slots.shape[2]
    assert width == LANES and LANES % capacity == 0
    assert unit_rows % (8 * groups) == 0 and unit_rows % TILE == 0
    hot_blocks, cold_blocks = hot_count // LANES, cold_count // LANES

    f32, i32, bf16 = jnp.float32, jnp.int32, jnp.bfloat16
    vmem, anywhere = pl.BlockSpec(memory_space=pltpu.VMEM), pl.BlockSpec(memory_space=pl.ANY)
    dma = pltpu.SemaphoreType.DMA
    results = pl.pallas_call(
        functools.partial(kernel, reps, shards),
        out_shape=(
            pltpu.VMEM((hot_blocks, LANES, LANES), f32),
            pltpu.VMEM((hot_blocks, 1, LANES), f32),
            pltpu.VMEM((cold_count, LANES), f32),
            pltpu.VMEM((cold_blocks, 1, LANES), f32),
        ),
        in_specs=[anywhere] * 9,
        out_specs=(vmem,) * 4,
        scratch_shapes=[
            pltpu.VMEM((2, 1, lookups), i32),
            pltpu.VMEM((2, lookups, LANES), bf16),
            pltpu.VMEM((UNITS, unit_rows, LANES), f32),
            pltpu.VMEM((UNITS, unit_rows, LANES), f32),
            pltpu.VMEM((2 * UNITS, unit_rows, LANES), f32),
            pltpu.VMEM((hot_blocks, 1, LANES), f32),
            pltpu.VMEM((cold_blocks, 1, LANES), f32),
            pltpu.VMEM((capacity, total), i32),
            pltpu.VMEM((1, total), i32),
            pltpu.VMEM((total, capacity, LANES), bf16),
            pltpu.VMEM((total, 1, LANES), i32),
            pltpu.VMEM((total, 1, LANES), i32),
            pltpu.VMEM((total, capacity, LANES), bf16),
            dma((10,)), dma((2,)), dma((2,)),
            dma((UNITS * steps,)), dma((UNITS * steps,)), dma((UNITS * steps,)), dma((UNITS * steps,)),
            dma((2 * UNITS,)), dma((2 * UNITS,)), dma((2,)), dma((2,)),
        ],
        compiler_params=pltpu.CompilerParams(
            collective_id=0, has_side_effects=True, vmem_limit_bytes=40 * 1024 * 1024
        ),
    )(
        hot_ids.reshape(1, lookups),
        hot_grads,
        hot_rows.reshape(hot_blocks, LANES, LANES),
        hot_accum.reshape(hot_blocks, 1, LANES),
        cold_slots.reshape(total, capacity).T,
        cold_counts,
        cold_grads.reshape(total, capacity, LANES),
        cold_rows,
        cold_accum.reshape(cold_blocks, 1, LANES),
    )
    results = [pltpu.with_memory_space_constraint(x, pltpu.VMEM) for x in results]
    hot_new, hot_accum_new, cold_new, cold_accum_new = pl.pallas_call(
        flush,
        out_shape=tuple(jax.ShapeDtypeStruct(x.shape, f32) for x in results),
        in_specs=[vmem] * 4,
        out_specs=(anywhere,) * 4,
        scratch_shapes=[dma((4,))],
        compiler_params=pltpu.CompilerParams(vmem_limit_bytes=16 * 1024 * 1024),
    )(*results)
    return (
        hot_new.reshape(hot_count, LANES),
        hot_accum_new.reshape(hot_count),
        cold_new,
        cold_accum_new.reshape(cold_count),
    )


def solution(mesh):
    placed = (
        P(BOTH), P(BOTH, None), P(), P(), P(BOTH, None), P(BOTH, None, None),
        P(BOTH, None, None, None), P(BOTH, None), P(BOTH),
    )
    return jax.shard_map(
        local,
        mesh=mesh,
        in_specs=placed,
        out_specs=(P(), P(), P(BOTH, None), P(BOTH)),
        check_vma=False,
    )
```

time: 85.4 us -> 81.1 us (0.950)
  other arithmetic: 2.1 us -> 0 us
  Pallas kernels: 74 us -> 72.3 us
    pallas_call x1 -> x2, Pallas kernels: 74 us -> 72.3 us  [the longest x1 68.8 us: local(): pl.pallas_call(functools.partial(kernel, reps, shards), out_shape=(pltpu....]
    select_n x1 -> x0, other arithmetic: 1.38 us -> none  [local(): cold_ids = jnp.where(live, slot_lanes + 1, 0)]
    unnamed x10 -> x16, local copies, waits for them, and re-layouts: 7.88 us -> 7.69 us
where the time goes in v1:
time: 81.1 us; the launch traced here: 80.6 us
  Pallas kernels  72.3 us (89%)
  local copies, waits for them, and re-layouts  7.69 us (9%)
    pallas_call x1, Pallas kernels, local(): pl.pallas_call(functools.partial(kernel, reps, shards), out_shape=(pltpu....  68.8 us
    unnamed x16, local copies, waits for them, and re-layouts  7.69 us
    pallas_call x1, Pallas kernels, local(): pl.pallas_call(flush, out_shape=tuple((jax.ShapeDtypeStruct(x.shape, f32)...  3.43 us

profile of v1, /device:TPU:0, one launch (start us, length us, event | category | flops | bytes accessed | tf_op | source)
XLA Modules:
  0.0 80.6 jit_solution(10505644909613572263)
XLA Ops:
  0.6 0.0 copy-start
  0.6 2.2 %copy-done = f32[8192,128]{1,0:T(8,128)S(1)} copy-done((f32[8192,128]{1,0:T(8,128)S(1)}, f32[8192,128]{1,0:T(8,128)}, u32[]{:S(2)}) %copy-start) | copy-done | bytes 4194328
  2.8 0.0 copy-start.1
  2.8 1.0 %copy-done.1 = bf16[2048,128]{1,0:T(8,128)(2,1)S(1)} copy-done((bf16[2048,128]{1,0:T(8,128)(2,1)S(1)}, bf16[2048,128]{1,0:T(8,128)(2,1)}, u32[]{:S(2)}) %copy-start.1) | copy-done | bytes 524312
  3.9 0.0 copy-start.2
  3.9 0.9 %copy-done.2 = bf16[1,32,16,128]{3,2,1,0:T(8,128)(2,1)S(1)} copy-done((bf16[1,32,16,128]{3,2,1,0:T(8,128)(2,1)S(1)}, bf16[1,32,16,128]{3,2,1,0:T(8,128)(2,1)}, u32[]{:S(2)}) %copy-start.2) | copy-done | bytes 131096
  4.8 0.0 copy-start.3
  4.8 0.8 copy-done.3
  5.5 0.0 copy-start.4
  5.5 0.8 copy-done.4
  6.3 0.0 copy-start.5
  6.3 0.7 copy-done.5
  7.0 0.0 copy-start.6
  7.0 0.7 copy-done.6
  7.7 0.0 copy-start.7
  7.7 0.7 copy-done.7
  8.3 68.8 %shard_map.120 = (f32[64,128,128]{2,1,0:T(8,128)S(1)}, f32[64,1,128]{2,1,0:T(1,128)S(1)}, f32[8192,128]{1,0:T(8,128)S(1)}, f32[64,1,128]{2,1,0:T(1,128)S(1)}) custom-call(s32[1,2048]{1,0:T(1,128)S(1)} %bitcast.15, bf16[2048,128]{1,0:T(8,128)(2,1)S(1)} %copy-done.1, f32[64,128,128]{2,1,0:T(8,128)S(1)} %bitcast.11, f32[64,1,128]{2,1,0:T(1,128)S(1)} %bitcast.13, ...), custom_call_target="tpu_custom_call" | custom-call | tf_op jit(solution)/shard_map/pallas_call | solution.py:328
  77.2 3.4 %shard_map.121 = (f32[64,128,128]{2,1,0:T(8,128)}, f32[64,1,128]{2,1,0:T(1,128)}, f32[8192,128]{1,0:T(8,128)}, f32[64,1,128]{2,1,0:T(1,128)}) custom-call(f32[64,128,128]{2,1,0:T(8,128)S(1)} %get-tuple-element.12.hot, f32[64,1,128]{2,1,0:T(1,128)S(1)} %get-tuple-element.13.hot_accum, f32[8192,128]{1,0:T(8,128)S(1)} %get-tuple-element.14.cold, ...), custom_call_target="tpu_custom_call" | custom-call | tf_op jit(solution)/shard_map/pallas_call | solution.py:371
Async XLA Ops:
  0.6 2.2 %copy-start = (f32[8192,128]{1,0:T(8,128)S(1)}, f32[8192,128]{1,0:T(8,128)}, u32[]{:S(2)}) copy-start(f32[8192,128]{1,0:T(8,128)} %param.11) | copy-start | bytes 12582916
  2.8 1.0 %copy-start.1 = (bf16[2048,128]{1,0:T(8,128)(2,1)S(1)}, bf16[2048,128]{1,0:T(8,128)(2,1)}, u32[]{:S(2)}) copy-start(bf16[2048,128]{1,0:T(8,128)(2,1)} %grads.1) | copy-start | bytes 1572868
  3.9 0.9 %copy-start.2 = (bf16[1,32,16,128]{3,2,1,0:T(8,128)(2,1)S(1)}, bf16[1,32,16,128]{3,2,1,0:T(8,128)(2,1)}, u32[]{:S(2)}) copy-start(bf16[1,32,16,128]{3,2,1,0:T(8,128)(2,1)} %param.15) | copy-start | bytes 393220
  4.8 0.8 copy-start.3
  5.5 0.8 copy-start.4
  6.3 0.7 copy-start.5
  7.0 0.7 copy-start.6
  7.7 0.7 copy-start.7
